TPU v7x, 32 devices: a whole 2x2x4 slice. The times are simulated.
32 devices in a mesh: row: 4 (over y, x), col: 8 (over z, core).
Axes of the slice: x: 2, y: 2, z: 4, core: 2. Of those that a mesh axis runs over, the one named last changes fastest.
Arguments:
- pair_states: bfloat16 [1024, 16384], P(None, ('row', 'col')), may hold values from -0.046875 to 0.046875
- screening: bfloat16 [4, 16384, 16384], P(None, 'row', 'col'), may hold values from -6 to 6
- qp_energy: float32 [8], replicated, may hold values from -0.5 to 0.5
- band_energy: float32 [2048], replicated, may hold values from -2 to 2
- band_index: int32 [128], replicated, may hold values from 0 to 2047
- nodes: float32 [4], replicated, may hold values from 0.1 to 2
- node_weights: float32 [4], replicated, may hold values from 0.05 to 1
Outputs:
- contrib: float32 [8, 128], replicated
- sigma: float32 [8], replicated
All inputs are finite; a program needn't handle non-finite values.
Results may differ from a plain program's by a relative error of at most 0.0003.
Values may be sent and summed in bfloat16 or wider, within the bound.
A program may use at most 128 MiB of HBM per device.

v0:
```python
import functools

import jax
import jax.numpy as jnp
from jax import lax
from jax.experimental import pallas as pl
from jax.experimental.pallas import tpu as pltpu
from jax.sharding import PartitionSpec as P

MESH = pl.DeviceIdType.MESH
CORES = 2


def orders(chips):
    table = []
    for here in range(chips):
        steps = [(here, 0), (here, 1)]
        for reach in range(1, chips):
            near = [other for other in (here - reach, here + reach) if 0 <= other < chips]
            steps += [(other, 0) for other in near] + [(other, 1) for other in near]
        table.append(steps)
    return table


def relay_steps(chips):
    return [2 * reach for reach in range(1, chips)]


def pick(table, row, column):
    value = jnp.int32(0)
    for i, line in enumerate(table):
        for j, entry in enumerate(line):
            if entry:
                value = jnp.where((row == i) & (column == j), jnp.int32(entry), value)
    return value


def kernel(
    rows, columns, own_ref, w_ref, factor_ref, out_ref,
    panel, cols, acc, tiles, quad, near_sum, far_sum,
    tile_sem, own_sem, send_sem, recv_sem, col_send, col_recv, near_send, near_recv, far_send, far_recv,
):
    row, column = lax.axis_index("row"), lax.axis_index("col")
    chips = columns // CORES
    chip, core = column // CORES, column % CORES
    partner = column + 1 - 2 * core
    freqs, _, width = w_ref.shape
    depth = own_ref.shape[1]
    pieces = width // depth
    pairs = own_ref.shape[0]
    table = orders(chips)
    steps = columns

    def at(r, c):
        return {"row": r, "col": c}

    barrier = pltpu.get_barrier_semaphore()
    linear = row * columns + column
    to_row, to_col = linear % pieces, linear // pieces
    stays = (to_row == row) & (to_col == column)
    first = row * 0 + column * pieces + row
    from_row, from_col = first // columns, first % columns
    for other in range(1, columns):
        pl.semaphore_signal(barrier, inc=1, device_id=at(row, (column + other) % columns), device_id_type=MESH)
    for other in range(1, rows):
        pl.semaphore_signal(barrier, inc=1, device_id=at((row + other) % rows, column), device_id_type=MESH)

    @pl.when(jnp.logical_not(stays))
    def _():
        pl.semaphore_signal(barrier, inc=1, device_id=at(to_row, to_col), device_id_type=MESH)
        pl.semaphore_signal(barrier, inc=1, device_id=at(from_row, from_col), device_id_type=MESH)

    def slot_of(step):
        source = pick([[s[0] for s in line] for line in table], chip, step)
        other = pick([[s[1] for s in line] for line in table], chip, step)
        return source * CORES + jnp.where(other == 1, 1 - core, core)

    def tile_copy(index):
        step, freq = index // freqs, index % freqs
        lines = pl.ds(pl.multiple_of(slot_of(step) * depth, depth), depth)
        spot = index % tiles.shape[0]
        return pltpu.make_async_copy(w_ref.at[freq, lines, :], tiles.at[spot], tile_sem.at[spot])

    ahead = tiles.shape[0] - 1
    for index in range(ahead):
        tile_copy(index).start()
    own_copy = pltpu.make_async_copy(own_ref, panel.at[column], own_sem)
    own_copy.start()

    pl.semaphore_wait(barrier, columns + rows - 2 + jnp.where(stays, 0, 2))
    own_copy.wait()

    def pass_on(source, way):
        slot = source * CORES + core
        target = [column + CORES, column - CORES, partner][way]
        return pltpu.make_async_remote_copy(
            src_ref=panel.at[slot], dst_ref=panel.at[slot], send_sem=send_sem.at[way, source],
            recv_sem=recv_sem.at[slot], device_id=at(row, target), device_id_type=MESH,
        )

    def goes(source, way):
        if way == 0:
            return (source <= chip) & (chip < chips - 1)
        return (source >= chip) & (chip > 0)

    def forward(source):
        for way in (0, 1):

            @pl.when(goes(source, way))
            def _():
                pass_on(source, way).start()

        pass_on(source, 2).start()

    def arrive(slot):
        pltpu.make_async_copy(panel.at[slot], panel.at[slot], recv_sem.at[slot]).wait()

    def col_first():
        return pltpu.make_async_remote_copy(
            src_ref=panel.at[column], dst_ref=cols.at[to_row], send_sem=col_send.at[0],
            recv_sem=col_recv.at[to_row], device_id=at(to_row, to_col), device_id_type=MESH,
        )

    def col_local():
        return pltpu.make_async_copy(panel.at[column], cols.at[row], col_recv.at[row])

    def col_next(other):
        return pltpu.make_async_remote_copy(
            src_ref=cols.at[row], dst_ref=cols.at[row], send_sem=col_send.at[other],
            recv_sem=col_recv.at[row], device_id=at((row + other) % rows, column), device_id_type=MESH,
        )

    def col_arrive(slot):
        pltpu.make_async_copy(cols.at[slot], cols.at[slot], col_recv.at[slot]).wait()

    forward(chip)

    @pl.when(jnp.logical_not(stays))
    def _():
        col_first().start()

    @pl.when(stays)
    def _():
        col_local().start()

    def product(slot, spot, piece):
        return jnp.dot(
            panel[slot], tiles[spot, :, pl.ds(pl.multiple_of(piece * depth, depth), depth)],
            preferred_element_type=jnp.float32,
        )

    def each(step, work):
        slot = slot_of(step)

        @pl.loop(0, freqs)
        def _(freq):
            index = step * freqs + freq
            spot = index % tiles.shape[0]

            @pl.when(index + ahead < steps * freqs)
            def _():
                tile_copy(index + ahead).start()

            tile_copy(index).wait()

            @pl.loop(0, pieces)
            def _(piece):
                work(freq, piece, product(slot, spot, piece))

    def at_piece(piece):
        return pl.ds(pl.multiple_of(piece * depth, depth), depth)

    def store(freq, piece, value):
        acc[freq, :, at_piece(piece)] = value

    def add(freq, piece, value):
        acc[freq, :, at_piece(piece)] += value

    def close(freq, piece, value):
        total = (acc[freq, :, at_piece(piece)] + value) * cols[piece].astype(jnp.float32)
        part = total[:, :128]
        for lane in range(128, depth, 128):
            part = part + total[:, lane : lane + 128]

        @pl.when(piece == 0)
        def _():
            quad[freq] = part

        @pl.when(piece > 0)
        def _():
            quad[freq] += part

    each(0, store)

    def sides(reach, work):
        for source in (chip - reach, chip + reach):

            @pl.when((source >= 0) & (source < chips))
            def _():
                work(source)

    def prepare(step):
        for reach, when in enumerate(relay_steps(chips), 1):

            @pl.when(step == when)
            def _():
                def one(source):
                    arrive(source * CORES + core)
                    forward(source)

                sides(reach, one)

        @pl.when(step == COL_STEP)
        def _():
            col_arrive(row)
            for other in range(1, rows):
                col_next(other).start()

        slot = slot_of(step)

        @pl.when(slot % CORES != core)
        def _():
            arrive(slot)

    @pl.loop(1, steps - 1)
    def _(step):
        prepare(step)
        each(step, add)

    prepare(steps - 1)
    for other in range(1, rows):
        col_arrive((row + other) % rows)
    each(steps - 1, close)

    bands = pairs // 128
    lines = []
    for band in range(bands):
        line = jnp.zeros((1, 128), jnp.float32)
        for freq in range(freqs):
            turned = quad[freq, pl.ds(band * 128, 128), :].T
            line = line + jnp.sum(turned, axis=0, keepdims=True) * factor_ref[freq, pl.ds(band, 1), :]
        lines.append(line)
    near_sum[column] = jnp.concatenate(lines, axis=0)

    def near(other):
        return pltpu.make_async_remote_copy(
            src_ref=near_sum.at[column], dst_ref=near_sum.at[column], send_sem=near_send.at[other],
            recv_sem=near_recv.at[column], device_id=at(row, (column + other) % columns), device_id_type=MESH,
        )

    def far(other):
        return pltpu.make_async_remote_copy(
            src_ref=far_sum.at[row], dst_ref=far_sum.at[row], send_sem=far_send.at[other],
            recv_sem=far_recv.at[row], device_id=at((row + other) % rows, column), device_id_type=MESH,
        )

    for other in range(1, columns):
        near(other).start()
    for other in range(1, columns):
        slot = (column + other) % columns
        pltpu.make_async_copy(near_sum.at[slot], near_sum.at[slot], near_recv.at[slot]).wait()
    total = near_sum[0]
    for slot in range(1, columns):
        total = total + near_sum[slot]
    far_sum[row] = total
    for other in range(1, rows):
        far(other).start()
    for other in range(1, rows):
        slot = (row + other) % rows
        pltpu.make_async_copy(far_sum.at[slot], far_sum.at[slot], far_recv.at[slot]).wait()
    total = far_sum[0]
    for slot in range(1, rows):
        total = total + far_sum[slot]
    out_ref[...] = total

    def sent(source):
        for way in (0, 1):

            @pl.when(goes(source, way))
            def _():
                pass_on(source, way).wait_send()

        pass_on(source, 2).wait_send()

    for source in range(chips):
        sent(source)

    @pl.when(jnp.logical_not(stays))
    def _():
        col_first().wait_send()

    for other in range(1, rows):
        col_next(other).wait_send()
        far(other).wait_send()
    for other in range(1, columns):
        near(other).wait_send()


def weights(qp_energy, band_energy, band_index, nodes, node_weights):
    table = lax.broadcasted_iota(jnp.int32, (band_index.shape[0], band_energy.shape[0]), 1)
    chosen = jnp.sum(
        jnp.where(band_index[:, None] == table, band_energy[None, :], jnp.float32(0.0)), axis=1
    )
    gap = (qp_energy[:, None] - chosen[None, :])[None]
    return node_weights[:, None, None] * gap / (gap * gap + (nodes * nodes)[:, None, None])


COL_STEP = 3


def fused(pair_states, screening, qp_energy, band_energy, band_index, nodes, node_weights):
    rows, columns = lax.axis_size("row"), lax.axis_size("col")
    pairs, depth = pair_states.shape
    freqs, _, width = screening.shape
    factor = weights(qp_energy, band_energy, band_index, nodes, node_weights)
    shape = (qp_energy.shape[0], band_index.shape[0])
    dma = pltpu.SemaphoreType.DMA
    contrib = pl.pallas_call(
        functools.partial(kernel, rows, columns),
        out_shape=jax.ShapeDtypeStruct(shape, jnp.float32),
        in_specs=[
            pl.BlockSpec(memory_space=pl.ANY),
            pl.BlockSpec(memory_space=pl.ANY),
            pl.BlockSpec(memory_space=pltpu.VMEM),
        ],
        out_specs=pl.BlockSpec(memory_space=pltpu.VMEM),
        scratch_shapes=[
            pltpu.VMEM((columns, pairs, depth), jnp.bfloat16),
            pltpu.VMEM((width // depth, pairs, depth), jnp.bfloat16),
            pltpu.VMEM((freqs, pairs, width), jnp.float32),
            pltpu.VMEM((3, depth, width), jnp.bfloat16),
            pltpu.VMEM((freqs, pairs, 128), jnp.float32),
            pltpu.VMEM((columns,) + shape, jnp.float32),
            pltpu.VMEM((rows,) + shape, jnp.float32),
            dma((3,)),
            dma,
            dma((3, columns // CORES)),
            dma((columns,)),
            dma((rows,)),
            dma((rows,)),
            dma((columns,)),
            dma((columns,)),
            dma((rows,)),
            dma((rows,)),
        ],
        compiler_params=pltpu.CompilerParams(
            collective_id=0, has_side_effects=True, vmem_limit_bytes=67043328
        ),
        cost_estimate=pl.CostEstimate(
            flops=2 * freqs * pairs * columns * depth * width,
            bytes_accessed=freqs * columns * depth * width * 2,
            transcendentals=0,
        ),
    )(pair_states, screening, factor)
    return contrib, jnp.sum(contrib, axis=1)


def broadcast(block, axis, holder):
    block = jnp.where(lax.axis_index(axis) == holder, block, jnp.zeros_like(block))
    return lax.psum(block, axis)


def shards(pair_states, screening, qp_energy, band_energy, band_index, nodes, node_weights):
    width = screening.shape[2]
    panel = lax.all_gather(pair_states, "col", axis=1, tiled=True)
    images = jnp.einsum("pg,fgc->fpc", panel, screening, preferred_element_type=jnp.float32)
    ratio = lax.axis_size("col") // lax.axis_size("row")
    column = lax.axis_index("col")
    offset = column % ratio * width
    own_piece = lax.dynamic_slice_in_dim(panel, offset, width, 1)
    col_states = broadcast(own_piece, "row", column // ratio)
    partial_value = jnp.sum(images * col_states.astype(jnp.float32)[None, :, :], axis=2)
    table = lax.broadcasted_iota(jnp.int32, (band_index.shape[0], band_energy.shape[0]), 1)
    chosen = jnp.sum(
        jnp.where(band_index[:, None] == table, band_energy[None, :], jnp.float32(0.0)), axis=1
    )
    gap = (qp_energy[:, None] - chosen[None, :]).reshape(-1)
    factor = (
        node_weights[:, None]
        * gap[None, :]
        / (gap[None, :] * gap[None, :] + nodes[:, None] * nodes[:, None])
    )
    flat = lax.psum(jnp.sum(factor * partial_value, axis=0), ("row", "col"))
    contrib = flat.reshape(qp_energy.shape[0], band_index.shape[0])
    sigma = jnp.sum(contrib, axis=1)
    return (contrib, sigma)


def step(pair_states, screening, *others):
    rows, columns = lax.axis_size("row"), lax.axis_size("col")
    pairs, depth = pair_states.shape
    freqs, _, width = screening.shape
    held = pairs * (columns * depth * 2 + width * 2 + freqs * width * 4 + freqs * 512) + 3 * depth * width * 2
    fits = depth % 128 == 0 and width == rows * depth and columns % CORES == 0 and held < 60 * 2**20
    fits = fits and others[2].shape[0] == 128 and columns >= 2 * CORES
    return (fused if fits else shards)(pair_states, screening, *others)


def solution(mesh):
    in_specs = (P(None, ("row", "col")), P(None, "row", "col"), P(), P(), P(), P(), P())
    out_specs = (P(), P())
    return jax.shard_map(step, mesh=mesh, in_specs=in_specs, out_specs=out_specs, check_vma=False)
```

profile of v0, /device:TPU:0, one launch (start us, length us, event | category | flops | bytes accessed | tf_op | source)
XLA Modules:
  0.0 184.8 jit_solution(17285373552223058375)
XLA Ops:
  0.6 0.9 select_reduce_fusion
  1.6 0.7 mul.28
  2.3 0.7 broadcast_subtract_fusion
  3.0 1.3 add_divide_fusion.factor_ref
  4.4 177.9 %shard_map.86 = f32[8,128]{1,0:T(8,128)} custom-call(bf16[1024,512]{1,0:T(8,128)(2,1)} %own_ref.1, bf16[4,4096,2048]{2,1,0:T(8,128)(2,1)} %w_ref.1, f32[4,8,128]{2,1,0:T(8,128)} %add_divide_fusion.factor_ref), custom_call_target="tpu_custom_call" | custom-call | flops 68719476736 | bytes 67108864 | tf_op jit(solution)/shard_map/pallas_call | solution.py:318
  182.2 1.3 reduce_sum.19
  183.5 1.3 copy.10
where the time goes:
time: 185 us
  Pallas kernels  178 us (96%)
  other arithmetic  5.04 us (3%)
    pallas_call x1, Pallas kernels, fused(): pl.pallas_call(functools.partial(kernel, rows, columns), out_shape=jax.Sh...  178 us

commit v1 on v0

v1 whole, which is shorter than its diff:
```python
import functools

import jax
import jax.numpy as jnp
from jax import lax
from jax.experimental import pallas as pl
from jax.experimental.pallas import tpu as pltpu
from jax.sharding import PartitionSpec as P

MESH = pl.DeviceIdType.MESH
CORES = 2
LANES = 128
RING = 4
CLOSE = 64

TAKE = {1: (4, 7, 9, 11), 2: (14, 16, 19, 20), 3: (24, 24, 28, 32)}
LATE = 99
PASS = (
    ((2, 4, 5, 6), (7, 10, 12, 14), (17, 19, 22, 23), (26, 27, 32, LATE)),
    ((4, 6, 7, 8), (10, 13, 15, 17), (20, 22, 25, 26), (28, 30, LATE, LATE)),
)


def kernel(
    rows, columns, own_ref, w_ref, qp_ref, band_ref, index_ref, nodes_ref, weights_ref, out_ref,
    panel, acc, tiles, qsum, fcol, chosen, near_sum, far_sum, qp, band, index, nodes, weights, taken, passed,
    small_sem, tile_sem, own_sem, r_send, r_recv, c_send, c_relay, c_recv, near_send, near_recv, far_send, far_recv,
):
    row, column = lax.axis_index("row"), lax.axis_index("col")
    chips = columns // CORES
    chip, core = column // CORES, column % CORES
    partner = column + 1 - 2 * core
    freqs, _, width = w_ref.shape
    pairs, depth = own_ref.shape
    parts = depth // LANES
    half = parts // 2
    steps = columns
    last = steps - 1
    units = steps * freqs + freqs
    bands = pairs // LANES
    held = columns * parts
    mine = width // LANES

    def at(r, c):
        return {"row": r, "col": c}

    home = chip
    side_x = home + 1 - 2 * (home % 2)
    side_y = (home + 2) % rows
    across = rows - 1 - home
    is_home = row == home
    ends = (chip == 0) | (chip == chips - 1)
    farthest = chips - 1 - chip
    is_x, is_y, is_far = row == side_x, row == side_y, row == across

    small = [
        pltpu.make_async_copy(src, dst, small_sem.at[i])
        for i, (src, dst) in enumerate(
            ((band_ref, band), (index_ref, index), (qp_ref, qp), (nodes_ref, nodes), (weights_ref, weights))
        )
    ]

    def rid(source, kind, part):
        return (source * CORES + kind) * parts + part

    def cid(source, kind, part):
        return ((source % CORES) * CORES + kind) * parts + part

    barrier = pltpu.get_barrier_semaphore()
    for other in range(1, columns):
        pl.semaphore_signal(barrier, inc=1, device_id=at(row, (column + other) % columns), device_id_type=MESH)
    for other in range(1, rows):
        for c in (column, partner):
            pl.semaphore_signal(barrier, inc=1, device_id=at((row + other) % rows, c), device_id_type=MESH)

    def own_copy(part):
        return pltpu.make_async_copy(
            own_ref.at[:, pl.ds(part * LANES, LANES)], panel.at[rid(chip, core, part)], own_sem.at[part]
        )

    for part in range(parts):
        own_copy(part).start()

    def source_of(step):
        j = step - 2
        edge = jnp.where(chip == 0, 1 + j // 2, chips - 2 - j // 2)
        inner = jnp.where(j < 4, chip - 1 + 2 * (j % 2), jnp.where(chip == 1, chips - 1, 0))
        source = jnp.where(ends, edge, inner)
        h = jnp.where(ends | (j >= 4), j % 2, j // 2)
        return source, h

    def blocks(step):
        source, h = source_of(step)
        first = step < 2
        kind = jnp.where(step == 1, 1 - core, core)
        a = jnp.where(first, rid(chip, kind, 0), rid(source, core, h * half))
        b = jnp.where(first, rid(chip, kind, half), rid(source, 1 - core, h * half))
        return a, b

    rows_of = half * LANES

    def tile_start(freq, pair):
        spot = freq % RING
        for place, block in enumerate(pair):
            pltpu.make_async_copy(
                w_ref.at[freq, pl.ds(pl.multiple_of(block * LANES, LANES), rows_of), :],
                tiles.at[spot, pl.ds(place * rows_of, rows_of), :],
                tile_sem.at[spot],
            ).start()

    def tile_wait(freq):
        spot = freq % RING
        pltpu.make_async_copy(tiles.at[spot], tiles.at[spot], tile_sem.at[spot]).wait()

    for freq in range(RING - 1):
        tile_start(freq, blocks(jnp.int32(0)))
    for copy in small:
        copy.start()

    def pass_on(source, part, way):
        slot = rid(source, core, part)
        target = [column + CORES, column - CORES, partner][way]
        return pltpu.make_async_remote_copy(
            src_ref=panel.at[slot], dst_ref=panel.at[slot], send_sem=r_send.at[way, source * parts + part],
            recv_sem=r_recv.at[slot], device_id=at(row, target), device_id_type=MESH,
        )

    def goes(source, way):
        if way == 0:
            return (source <= chip) & (chip < chips - 1)
        return (source >= chip) & (chip > 0)

    def c_first(source, part, side=0):
        slot = held + cid(source, core, part)
        return pltpu.make_async_remote_copy(
            src_ref=panel.at[rid(source, core, part)], dst_ref=panel.at[slot],
            send_sem=c_send.at[side, source * parts + part], recv_sem=c_recv.at[cid(source, core, part)],
            device_id=at(jnp.where(core == side, side_x, side_y), chip * CORES + source // CORES), device_id_type=MESH,
        )

    def c_next(kind, number):
        target = jnp.where(is_far, side_y if kind == 0 else side_x, across)
        return pltpu.make_async_remote_copy(
            src_ref=panel.at[held + number], dst_ref=panel.at[held + number], send_sem=c_relay.at[number],
            recv_sem=c_recv.at[number], device_id=at(target, column), device_id_type=MESH,
        )


    def relays(kind, source):
        return (is_far & (jnp.abs(source - chip) < chips - 1)) | (is_x if kind == 0 else is_y)

    def arrive(slot):
        pltpu.make_async_copy(panel.at[slot], panel.at[slot], r_recv.at[slot]).wait()

    def c_arrive(number):
        pltpu.make_async_copy(panel.at[held + number], panel.at[held + number], c_recv.at[number]).wait()

    def dispatch(source, part):
        for way in (0, 1):

            @pl.when(goes(source, way))
            def _():
                pass_on(source, part, way).start()

        pass_on(source, part, 2).start()

        @pl.when(is_home)
        def _():
            c_first(source, part).start()

    near_first = jnp.where(chip > core * CORES, 1, 0)
    wanted = [core * CORES + near_first, core * CORES + 1 - near_first]
    away = [jnp.abs(source - chip) for source in wanted]

    def due_at(order, part):
        value = jnp.int32(LATE)
        for distance in range(chips):
            there = jnp.where(is_far, PASS[1][distance][part], PASS[0][distance][part])
            value = jnp.where(away[order] == distance, there, value)
        return value

    due = [due_at(order, part) for order in range(2) for part in range(parts)]
    taken[units + 1] = jnp.int32(sum(map(len, TAKE.values())))
    for unit in range(units + 1):
        taken[unit] = jnp.int32(sum(take < unit for line in TAKE.values() for take in line))
        passed[unit] = sum((d < unit).astype(jnp.int32) for d in due)

    def wanted_at(order):
        return jnp.where(order == 0, wanted[0], wanted[1])

    def events(unit):
        @pl.loop(taken[unit], taken[unit + 1])
        def _(k):
            distance, part = 1 + k // parts, k % parts
            for source in (chip - distance, chip + distance):

                @pl.when((source >= 0) & (source < chips))
                def _():
                    arrive(rid(source, core, part))
                    dispatch(source, part)

        @pl.loop(passed[unit], passed[unit + 1])
        def _(k):
            for kind in range(CORES):

                @pl.when(relays(kind, wanted_at(k // parts)))
                def _():
                    number = cid(wanted_at(k // parts), kind, k % parts)
                    c_arrive(number)
                    c_next(kind, number).start()

        @pl.when(is_home & ends)
        def _():
            @pl.loop(taken[jnp.maximum(unit - 1, 0)], taken[unit])
            def _(k):
                @pl.when(k // parts == chips - 2)
                def _():
                    c_first(farthest, k % parts, 1).start()

    for copy in small:
        copy.wait()

    @pl.loop(0, LANES)
    def _(m):
        chosen[pl.ds(m, 1), :] = jnp.full((1, LANES), band[index[m]], jnp.float32)

    for freq in range(freqs):

        @pl.loop(0, bands)
        def _(n):
            gap = qp[n] - chosen[...]
            value = weights[freq] * gap / (gap * gap + nodes[freq] * nodes[freq])
            fcol[freq, pl.ds(pl.multiple_of(n * LANES, LANES), LANES), :] = value

    for part in range(parts):
        own_copy(part).wait()
    pl.semaphore_wait(barrier, columns - 1 + 2 * (rows - 1))
    for part in range(parts):
        dispatch(chip, part)

    def whole(freq, a, b):
        left = jnp.concatenate([panel[a + j] for j in range(half)] + [panel[b + j] for j in range(half)], axis=1)
        return jnp.dot(left, tiles[freq % RING], preferred_element_type=jnp.float32)

    def ahead(freq, pair, later):
        target = [jnp.where(freq == 0, now, then) for now, then in zip(pair, later)]
        tile_start((freq + RING - 1) % freqs, target)

    @pl.loop(0, freqs)
    def _(freq):
        events(freq)
        pair = blocks(jnp.int32(0))
        ahead(freq, pair, blocks(jnp.int32(1)))
        tile_wait(freq)
        acc[freq] = whole(freq, *pair)

    @pl.loop(1, last)
    def _(step):
        a, b = pair = blocks(step)
        later = blocks(step + 1)

        @pl.loop(0, freqs)
        def _(freq):
            events(step * freqs + freq)

            @pl.when(freq == 0)
            def _():
                @pl.when(step == 1)
                def _():
                    for j in range(half):
                        arrive(a + j)

                for j in range(half):
                    arrive(b + j)

            ahead(freq, pair, later)
            tile_wait(freq)
            acc[freq] += whole(freq, a, b)

    a, b = blocks(jnp.int32(last))
    for j in range(half):

        @pl.loop(0, freqs)
        def _(freq):
            events(last * freqs + j * freqs + freq)

            @pl.when(freq == 0)
            def _():
                arrive(b + j)

            if j == 0:

                @pl.when(freq == 0)
                def _():
                    tile_start(RING - 1, (a, b))

                tile_wait(freq)
            left = jnp.concatenate([panel[a + j], panel[b + j]], axis=1)
            spot = freq % RING
            right = jnp.concatenate(
                [tiles[spot, pl.ds(i * rows_of + j * LANES, LANES), :] for i in range(2)], axis=0
            )
            acc[freq] += jnp.dot(left, right, preferred_element_type=jnp.float32)

    base = jnp.where(is_home, core * mine, held)
    qsum[...] = jnp.zeros_like(qsum)

    def relay(order, part):
        for kind in range(CORES):

            @pl.when(relays(kind, wanted[order]) & (order * parts + part >= passed[units]))
            def _():
                number = cid(wanted[order], kind, part)
                c_arrive(number)
                c_next(kind, number).start()

    def collect(order, part):
        for kind in range(CORES):

            @pl.when(jnp.logical_not(is_home | relays(kind, wanted[order])))
            def _():
                c_arrive(cid(wanted[order], kind, part))

    def close(order, some):
        numbers = [cid(wanted[order], kind, part) for part in some for kind in range(CORES)]

        @pl.loop(0, pairs // CLOSE)
        def _(n):
            for i in range(0, CLOSE, 16):
                lines = pl.ds(pl.multiple_of(n * CLOSE, CLOSE) + i, 16)
                factors = [fcol[freq, lines, :] for freq in range(freqs)]
                value = qsum[lines, :]
                for number in numbers:
                    lanes = pl.ds(pl.multiple_of(number * LANES, LANES), LANES)
                    total = factors[0] * acc[0, lines, lanes]
                    for freq in range(1, freqs):
                        total = total + factors[freq] * acc[freq, lines, lanes]
                    value = value + total * panel[base + number, lines, :].astype(jnp.float32)
                qsum[lines, :] = value

    for order in range(2):
        for part in range(parts - order):
            relay(order, part)
    for part in range(parts):
        collect(0, part)
    close(0, range(parts))
    relay(1, parts - 1)
    for part in range(parts - 1):
        collect(1, part)
    close(1, range(parts - 1))
    collect(1, parts - 1)
    close(1, range(parts - 1, parts))

    sums = []
    for n in range(bands):
        sums.append(jnp.sum(qsum[pl.ds(n * LANES, LANES), :].T, axis=0, keepdims=True))
    near_sum[column] = jnp.concatenate(sums, axis=0)

    def near(other):
        return pltpu.make_async_remote_copy(
            src_ref=near_sum.at[column], dst_ref=near_sum.at[column], send_sem=near_send.at[other],
            recv_sem=near_recv.at[column], device_id=at(row, (column + other) % columns), device_id_type=MESH,
        )

    def far(other):
        return pltpu.make_async_remote_copy(
            src_ref=far_sum.at[row], dst_ref=far_sum.at[row], send_sem=far_send.at[other],
            recv_sem=far_recv.at[row], device_id=at((row + other) % rows, column), device_id_type=MESH,
        )

    for other in range(1, columns):
        near(other).start()
    for other in range(1, columns):
        slot = (column + other) % columns
        pltpu.make_async_copy(near_sum.at[slot], near_sum.at[slot], near_recv.at[slot]).wait()
    total = near_sum[0]
    for slot in range(1, columns):
        total = total + near_sum[slot]
    far_sum[row] = total
    for other in range(1, rows):
        far(other).start()
    for other in range(1, rows):
        slot = (row + other) % rows
        pltpu.make_async_copy(far_sum.at[slot], far_sum.at[slot], far_recv.at[slot]).wait()
    total = far_sum[0]
    for slot in range(1, rows):
        total = total + far_sum[slot]
    out_ref[...] = total

    for source in range(chips):

        @pl.loop(0, parts)
        def _(part):
            for way in (0, 1):

                @pl.when(goes(source, way))
                def _():
                    pass_on(source, part, way).wait_send()

            pass_on(source, part, 2).wait_send()

            @pl.when(is_home)
            def _():
                c_first(source, part).wait_send()

    @pl.when(is_home & ends)
    def _():
        @pl.loop(0, parts)
        def _(part):
            c_first(farthest, part, 1).wait_send()

    for kind in range(CORES):
        for order in range(2):

            @pl.when(relays(kind, wanted[order]))
            def _():
                @pl.loop(0, parts)
                def _(part):
                    c_next(kind, cid(wanted[order], kind, part)).wait_send()

    for other in range(1, rows):
        far(other).wait_send()
    for other in range(1, columns):
        near(other).wait_send()


def fused(pair_states, screening, qp_energy, band_energy, band_index, nodes, node_weights):
    rows, columns = lax.axis_size("row"), lax.axis_size("col")
    pairs, depth = pair_states.shape
    freqs, _, width = screening.shape
    shape = (qp_energy.shape[0], band_index.shape[0])
    parts = depth // LANES
    chips = columns // CORES
    mine = width // LANES
    dma = pltpu.SemaphoreType.DMA
    contrib = pl.pallas_call(
        functools.partial(kernel, rows, columns),
        out_shape=jax.ShapeDtypeStruct(shape, jnp.float32),
        in_specs=[pl.BlockSpec(memory_space=pl.ANY)] * 7,
        out_specs=pl.BlockSpec(memory_space=pltpu.VMEM),
        scratch_shapes=[
            pltpu.VMEM((columns * parts + mine, pairs, LANES), jnp.bfloat16),
            pltpu.VMEM((freqs, pairs, width), jnp.float32),
            pltpu.VMEM((RING, depth, width), jnp.bfloat16),
            pltpu.VMEM((pairs, LANES), jnp.float32),
            pltpu.VMEM((freqs, pairs, LANES), jnp.float32),
            pltpu.VMEM((LANES, LANES), jnp.float32),
            pltpu.VMEM((columns,) + shape, jnp.float32),
            pltpu.VMEM((rows,) + shape, jnp.float32),
            pltpu.SMEM(qp_energy.shape, jnp.float32),
            pltpu.SMEM(band_energy.shape, jnp.float32),
            pltpu.SMEM(band_index.shape, jnp.int32),
            pltpu.SMEM(nodes.shape, jnp.float32),
            pltpu.SMEM(node_weights.shape, jnp.float32),
            pltpu.SMEM((columns * freqs + freqs + 2,), jnp.int32),
            pltpu.SMEM((columns * freqs + freqs + 2,), jnp.int32),
            dma((5,)),
            dma((RING,)),
            dma((parts,)),
            dma((3, chips * parts)),
            dma((columns * parts,)),
            dma((2, chips * parts)),
            dma((mine,)),
            dma((mine,)),
            dma((columns,)),
            dma((columns,)),
            dma((rows,)),
            dma((rows,)),
        ],
        compiler_params=pltpu.CompilerParams(
            collective_id=0, has_side_effects=True, vmem_limit_bytes=67043328
        ),
        cost_estimate=pl.CostEstimate(
            flops=2 * freqs * pairs * columns * depth * width,
            bytes_accessed=freqs * columns * depth * width * 2,
            transcendentals=0,
        ),
    )(pair_states, screening, qp_energy, band_energy, band_index, nodes, node_weights)
    return contrib, jnp.sum(contrib, axis=1)


def broadcast(block, axis, holder):
    block = jnp.where(lax.axis_index(axis) == holder, block, jnp.zeros_like(block))
    return lax.psum(block, axis)


def shards(pair_states, screening, qp_energy, band_energy, band_index, nodes, node_weights):
    width = screening.shape[2]
    panel = lax.all_gather(pair_states, "col", axis=1, tiled=True)
    images = jnp.einsum("pg,fgc->fpc", panel, screening, preferred_element_type=jnp.float32)
    ratio = lax.axis_size("col") // lax.axis_size("row")
    column = lax.axis_index("col")
    offset = column % ratio * width
    own_piece = lax.dynamic_slice_in_dim(panel, offset, width, 1)
    col_states = broadcast(own_piece, "row", column // ratio)
    partial_value = jnp.sum(images * col_states.astype(jnp.float32)[None, :, :], axis=2)
    table = lax.broadcasted_iota(jnp.int32, (band_index.shape[0], band_energy.shape[0]), 1)
    chosen = jnp.sum(
        jnp.where(band_index[:, None] == table, band_energy[None, :], jnp.float32(0.0)), axis=1
    )
    gap = (qp_energy[:, None] - chosen[None, :]).reshape(-1)
    factor = (
        node_weights[:, None]
        * gap[None, :]
        / (gap[None, :] * gap[None, :] + nodes[:, None] * nodes[:, None])
    )
    flat = lax.psum(jnp.sum(factor * partial_value, axis=0), ("row", "col"))
    contrib = flat.reshape(qp_energy.shape[0], band_index.shape[0])
    sigma = jnp.sum(contrib, axis=1)
    return (contrib, sigma)


def step(pair_states, screening, *others):
    rows, columns = lax.axis_size("row"), lax.axis_size("col")
    pairs, depth = pair_states.shape
    freqs, _, width = screening.shape
    chips = columns // CORES
    held = pairs * ((columns * depth + width) * 2 + freqs * width * 4 + (freqs + 1) * LANES * 4)
    held = held + RING * depth * width * 2
    fits = depth == 4 * LANES and width == rows * depth and rows == 4 and chips == rows and columns % CORES == 0
    fits = fits and freqs == RING and others[2].shape[0] == LANES and pairs == others[0].shape[0] * LANES
    fits = fits and held < 60 * 2**20
    return (fused if fits else shards)(pair_states, screening, *others)


def solution(mesh):
    in_specs = (P(None, ("row", "col")), P(None, "row", "col"), P(), P(), P(), P(), P())
    out_specs = (P(), P())
    return jax.shard_map(step, mesh=mesh, in_specs=in_specs, out_specs=out_specs, check_vma=False)
```

time: 185 us -> 114 us (0.62)
  Pallas kernels: 178 us -> 111 us
  other arithmetic: 5.04 us -> 1.31 us
    pallas_call x1, Pallas kernels: 178 us -> 111 us  [fused(): pl.pallas_call(functools.partial(kernel, rows, columns), out_shape=jax.Sh...]
where the time goes in v1:
time: 114 us
  Pallas kernels  111 us (97%)
  other arithmetic  1.31 us (1%)
  local copies, waits for them, and re-layouts  1.27 us (1%)
    pallas_call x1, Pallas kernels, fused(): pl.pallas_call(functools.partial(kernel, rows, columns), out_shape=jax.Sh...  111 us

profile of v1, /device:TPU:0, one launch (start us, length us, event | category | flops | bytes accessed | tf_op | source)
XLA Modules:
  0.0 113.8 jit_solution(17102187404358434038)
XLA Ops:
  0.6 110.6 %shard_map.86 = f32[8,128]{1,0:T(8,128)} custom-call(bf16[1024,512]{1,0:T(8,128)(2,1)} %own_ref.1, bf16[4,4096,2048]{2,1,0:T(8,128)(2,1)} %w_ref.1, f32[8]{0:T(128)} %qp_ref.1, f32[2048]{0:T(1024)} %band_ref.1, s32[128]{0:T(128)} %index_ref.1, f32[4]{0:T(128)} %nodes_ref.1, f32[4]{0:T(128)} %weights_ref.1), custom_call_target="tpu_custom_call" | custom-call | flops 68719476736 | bytes 67108864 | tf_op jit(solution)/shard_map/pallas_call | solution.py:436
  111.2 1.3 %reduce_sum.9 = f32[8]{0:T(128)} reduce(f32[8,128]{1,0:T(8,128)} %shard_map.86, f32[]{:T(128)} %constant.0.clone.1), dimensions={1}, to_apply=%region_0.0 | reduce | flops 1016 | bytes 4132 | tf_op jit(solution)/shard_map/reduce_sum | solution.py:479
  112.5 1.3 %copy.10 = f32[8,128]{1,0:T(8,128)} copy(f32[8,128]{1,0:T(8,128)} %shard_map.86) | data formatting | bytes 8192

commit v2 on v1

--- a/solution.py
+++ b/solution.py
@@ -11,20 +11,21 @@
 CORES = 2
 LANES = 128
 RING = 4
-CLOSE = 64
-
-TAKE = {1: (4, 7, 9, 11), 2: (14, 16, 19, 20), 3: (24, 24, 28, 32)}
+CLOSE = 256
+PAIR = 2
+
+TAKE = {1: (4, 6, 8, 10), 2: (14, 16, 18, 20), 3: (22, 26, 30, 34)}
 LATE = 99
 PASS = (
-    ((2, 4, 5, 6), (7, 10, 12, 14), (17, 19, 22, 23), (26, 27, 32, LATE)),
-    ((4, 6, 7, 8), (10, 13, 15, 17), (20, 22, 25, 26), (28, 30, LATE, LATE)),
+    ((2, 4, 4, 6), (8, 10, 12, 14), (18, 20, 22, 24), (26, 30, 34, 38)),
+    ((4, 6, 8, 10), (10, 12, 14, 16), (22, 24, 26, 30), (30, 34, LATE, LATE)),
 )
 
 
 def kernel(
     rows, columns, own_ref, w_ref, qp_ref, band_ref, index_ref, nodes_ref, weights_ref, out_ref,
-    panel, acc, tiles, qsum, fcol, chosen, near_sum, far_sum, qp, band, index, nodes, weights, taken, passed,
-    small_sem, tile_sem, own_sem, r_send, r_recv, c_send, c_relay, c_recv, near_send, near_recv, far_send, far_recv,
+    panel, acc, tiles, qsum, fcol, chosen, total_of, qp, band, index, nodes, weights, taken, passed,
+    small_sem, tile_sem, own_sem, r_send, r_recv, c_send, c_relay, c_recv, tell_send, tell_recv,
 ):
     row, column = lax.axis_index("row"), lax.axis_index("col")
     chips = columns // CORES
@@ -36,7 +37,8 @@
     half = parts // 2
     steps = columns
     last = steps - 1
-    units = steps * freqs + freqs
+    halved = last - 1
+    units = (steps + steps - halved) * freqs
     bands = pairs // LANES
     held = columns * parts
     mine = width // LANES
@@ -112,10 +114,7 @@
         spot = freq % RING
         pltpu.make_async_copy(tiles.at[spot], tiles.at[spot], tile_sem.at[spot]).wait()
 
-    for freq in range(RING - 1):
-        tile_start(freq, blocks(jnp.int32(0)))
-    for copy in small:
-        copy.start()
+    tile_start(0, blocks(jnp.int32(0)))
 
     def pass_on(source, part, way):
         slot = rid(source, core, part)
@@ -146,8 +145,8 @@
         )
 
 
-    def relays(kind, source):
-        return (is_far & (jnp.abs(source - chip) < chips - 1)) | (is_x if kind == 0 else is_y)
+    def relays(kind, source, part):
+        return (is_far & ((jnp.abs(source - chip) < chips - 1) | (part < half))) | (is_x if kind == 0 else is_y)
 
     def arrive(slot):
         pltpu.make_async_copy(panel.at[slot], panel.at[slot], r_recv.at[slot]).wait()
@@ -203,7 +202,7 @@
         def _(k):
             for kind in range(CORES):
 
-                @pl.when(relays(kind, wanted_at(k // parts)))
+                @pl.when(relays(kind, wanted_at(k // parts), k % parts))
                 def _():
                     number = cid(wanted_at(k // parts), kind, k % parts)
                     c_arrive(number)
@@ -211,32 +210,20 @@
 
         @pl.when(is_home & ends)
         def _():
-            @pl.loop(taken[jnp.maximum(unit - 1, 0)], taken[unit])
+            @pl.loop(taken[jnp.maximum(unit - PAIR, 0)], taken[jnp.maximum(unit - 1, 0)])
             def _(k):
-                @pl.when(k // parts == chips - 2)
+                @pl.when((k // parts == chips - 2) & (k % parts >= half))
                 def _():
                     c_first(farthest, k % parts, 1).start()
-
-    for copy in small:
-        copy.wait()
-
-    @pl.loop(0, LANES)
-    def _(m):
-        chosen[pl.ds(m, 1), :] = jnp.full((1, LANES), band[index[m]], jnp.float32)
-
-    for freq in range(freqs):
-
-        @pl.loop(0, bands)
-        def _(n):
-            gap = qp[n] - chosen[...]
-            value = weights[freq] * gap / (gap * gap + nodes[freq] * nodes[freq])
-            fcol[freq, pl.ds(pl.multiple_of(n * LANES, LANES), LANES), :] = value
 
     for part in range(parts):
         own_copy(part).wait()
     pl.semaphore_wait(barrier, columns - 1 + 2 * (rows - 1))
     for part in range(parts):
         dispatch(chip, part)
+    tile_start(1, blocks(jnp.int32(0)))
+    for copy in small:
+        copy.start()
 
     def whole(freq, a, b):
         left = jnp.concatenate([panel[a + j] for j in range(half)] + [panel[b + j] for j in range(half)], axis=1)
@@ -244,24 +231,45 @@
 
     def ahead(freq, pair, later):
         target = [jnp.where(freq == 0, now, then) for now, then in zip(pair, later)]
-        tile_start((freq + RING - 1) % freqs, target)
-
-    @pl.loop(0, freqs)
+        for i in range(PAIR):
+            tile_start((freq + i + PAIR) % freqs, target)
+
+    @pl.loop(0, freqs, step=PAIR)
     def _(freq):
-        events(freq)
+        for i in range(PAIR):
+            events(freq + i)
         pair = blocks(jnp.int32(0))
         ahead(freq, pair, blocks(jnp.int32(1)))
-        tile_wait(freq)
-        acc[freq] = whole(freq, *pair)
-
-    @pl.loop(1, last)
+        for i in range(PAIR):
+            tile_wait(freq + i)
+        for i in range(PAIR):
+            acc[freq + i] = whole(freq + i, *pair)
+
+    for copy in small:
+        copy.wait()
+
+    @pl.loop(0, LANES, step=16)
+    def _(m):
+        for i in range(16):
+            chosen[pl.ds(m + i, 1), :] = jnp.full((1, LANES), band[index[m + i]], jnp.float32)
+
+    @pl.loop(0, bands)
+    def _(n):
+        gap = qp[n] - chosen[...]
+        square = gap * gap
+        for freq in range(freqs):
+            value = weights[freq] * gap / (square + nodes[freq] * nodes[freq])
+            fcol[freq, pl.ds(pl.multiple_of(n * LANES, LANES), LANES), :] = value
+
+    @pl.loop(1, halved)
     def _(step):
         a, b = pair = blocks(step)
         later = blocks(step + 1)
 
-        @pl.loop(0, freqs)
+        @pl.loop(0, freqs, step=PAIR)
         def _(freq):
-            events(step * freqs + freq)
+            for i in range(PAIR):
+                events(step * freqs + freq + i)
 
             @pl.when(freq == 0)
             def _():
@@ -274,33 +282,52 @@
                     arrive(b + j)
 
             ahead(freq, pair, later)
-            tile_wait(freq)
-            acc[freq] += whole(freq, a, b)
-
-    a, b = blocks(jnp.int32(last))
-    for j in range(half):
-
-        @pl.loop(0, freqs)
-        def _(freq):
-            events(last * freqs + j * freqs + freq)
-
-            @pl.when(freq == 0)
-            def _():
-                arrive(b + j)
-
-            if j == 0:
+            for i in range(PAIR):
+                tile_wait(freq + i)
+            for i in range(PAIR):
+                acc[freq + i] += whole(freq + i, a, b)
+
+    def left_of(pair, j):
+        return jnp.concatenate([panel[block + j] for block in pair], axis=1)
+
+    def right_of(freq, j, lanes):
+        return jnp.concatenate(
+            [tiles[freq % RING, pl.ds(i * rows_of + j * LANES, LANES), lanes] for i in range(2)], axis=0
+        )
+
+    pair, later = blocks(jnp.int32(halved)), blocks(jnp.int32(last))
+    for turn, now in ((0, pair), (half, later)):
+        for j in range(half if turn == 0 else half - 1):
+
+            @pl.loop(0, freqs, step=PAIR)
+            def _(freq):
+                for i in range(PAIR):
+                    events((halved + turn + j) * freqs + freq + i)
 
                 @pl.when(freq == 0)
                 def _():
-                    tile_start(RING - 1, (a, b))
-
-                tile_wait(freq)
-            left = jnp.concatenate([panel[a + j], panel[b + j]], axis=1)
-            spot = freq % RING
-            right = jnp.concatenate(
-                [tiles[spot, pl.ds(i * rows_of + j * LANES, LANES), :] for i in range(2)], axis=0
-            )
-            acc[freq] += jnp.dot(left, right, preferred_element_type=jnp.float32)
+                    arrive(now[1] + j)
+
+                if j == 0:
+
+                    @pl.when(freq == 0)
+                    def _():
+                        for i in range(PAIR):
+                            tile_start(PAIR + i, now)
+
+                    for i in range(PAIR):
+                        tile_wait(freq + i)
+                else:
+
+                    @pl.when(freq > 0)
+                    def _():
+                        for i in range(PAIR):
+                            tile_start(i, later)
+
+                for i in range(PAIR):
+                    acc[freq + i] += jnp.dot(
+                        left_of(now, j), right_of(freq + i, j, slice(None)), preferred_element_type=jnp.float32
+                    )
 
     base = jnp.where(is_home, core * mine, held)
     qsum[...] = jnp.zeros_like(qsum)
@@ -308,7 +335,7 @@
     def relay(order, part):
         for kind in range(CORES):
 
-            @pl.when(relays(kind, wanted[order]) & (order * parts + part >= passed[units]))
+            @pl.when(relays(kind, wanted[order], part) & (order * parts + part >= passed[units]))
             def _():
                 number = cid(wanted[order], kind, part)
                 c_arrive(number)
@@ -317,75 +344,71 @@
     def collect(order, part):
         for kind in range(CORES):
 
-            @pl.when(jnp.logical_not(is_home | relays(kind, wanted[order])))
+            @pl.when(jnp.logical_not(is_home | relays(kind, wanted[order], part)))
             def _():
                 c_arrive(cid(wanted[order], kind, part))
 
-    def close(order, some):
-        numbers = [cid(wanted[order], kind, part) for part in some for kind in range(CORES)]
-
-        @pl.loop(0, pairs // CLOSE)
+    arrive(later[1] + half - 1)
+    for order in range(2):
+        ready = parts - order
+        for part in range(ready):
+
+            @pl.when(passed[units] <= order * parts + part)
+            def _():
+                relay(order, part)
+
+            collect(order, part)
+
+        @pl.loop(0, CORES)
+        def _(kind):
+            events((last + half) * freqs + order * CORES + kind)
+            number = cid(wanted[order], kind, 0)
+            lanes = pl.ds(pl.multiple_of(number * LANES, LANES), depth)
+            for freq in range(freqs):
+                value = acc[freq, :, lanes] + jnp.dot(
+                    left_of(later, half - 1), right_of(freq, half - 1, lanes), preferred_element_type=jnp.float32
+                )
+                part_sum = value[:, :LANES] * panel[base + number].astype(jnp.float32)
+                for part in range(1, ready):
+                    piece = value[:, part * LANES : (part + 1) * LANES]
+                    part_sum = part_sum + piece * panel[base + number + part].astype(jnp.float32)
+                for part in range(ready, parts):
+                    piece = fcol[freq] * value[:, part * LANES : (part + 1) * LANES]
+                    spot = pl.ds(pl.multiple_of((number + part) * LANES, LANES), LANES)
+                    if freq == 0:
+                        acc[0, :, spot] = piece
+                    else:
+                        acc[0, :, spot] += piece
+                qsum[...] += fcol[freq] * part_sum
+
+    relay(1, parts - 1)
+    collect(1, parts - 1)
+    for kind in range(CORES):
+        number = cid(wanted[1], kind, parts - 1)
+
+        @pl.loop(0, pairs, step=CLOSE)
         def _(n):
-            for i in range(0, CLOSE, 16):
-                lines = pl.ds(pl.multiple_of(n * CLOSE, CLOSE) + i, 16)
-                factors = [fcol[freq, lines, :] for freq in range(freqs)]
-                value = qsum[lines, :]
-                for number in numbers:
-                    lanes = pl.ds(pl.multiple_of(number * LANES, LANES), LANES)
-                    total = factors[0] * acc[0, lines, lanes]
-                    for freq in range(1, freqs):
-                        total = total + factors[freq] * acc[freq, lines, lanes]
-                    value = value + total * panel[base + number, lines, :].astype(jnp.float32)
-                qsum[lines, :] = value
-
-    for order in range(2):
-        for part in range(parts - order):
-            relay(order, part)
-    for part in range(parts):
-        collect(0, part)
-    close(0, range(parts))
-    relay(1, parts - 1)
-    for part in range(parts - 1):
-        collect(1, part)
-    close(1, range(parts - 1))
-    collect(1, parts - 1)
-    close(1, range(parts - 1, parts))
+            lines = pl.ds(pl.multiple_of(n, CLOSE), CLOSE)
+            spot = pl.ds(pl.multiple_of(number * LANES, LANES), LANES)
+            qsum[lines, :] += acc[0, lines, spot] * panel[base + number, lines, :].astype(jnp.float32)
 
     sums = []
     for n in range(bands):
         sums.append(jnp.sum(qsum[pl.ds(n * LANES, LANES), :].T, axis=0, keepdims=True))
-    near_sum[column] = jnp.concatenate(sums, axis=0)
-
-    def near(other):
+    everyone = rows * columns
+    linear = row * columns + column
+    total_of[linear] = jnp.concatenate(sums, axis=0)
+
+    def tell(other):
+        target = (linear + other) % everyone
         return pltpu.make_async_remote_copy(
-            src_ref=near_sum.at[column], dst_ref=near_sum.at[column], send_sem=near_send.at[other],
-            recv_sem=near_recv.at[column], device_id=at(row, (column + other) % columns), device_id_type=MESH,
-        )
-
-    def far(other):
-        return pltpu.make_async_remote_copy(
-            src_ref=far_sum.at[row], dst_ref=far_sum.at[row], send_sem=far_send.at[other],
-            recv_sem=far_recv.at[row], device_id=at((row + other) % rows, column), device_id_type=MESH,
-        )
-
-    for other in range(1, columns):
-        near(other).start()
-    for other in range(1, columns):
-        slot = (column + other) % columns
-        pltpu.make_async_copy(near_sum.at[slot], near_sum.at[slot], near_recv.at[slot]).wait()
-    total = near_sum[0]
-    for slot in range(1, columns):
-        total = total + near_sum[slot]
-    far_sum[row] = total
-    for other in range(1, rows):
-        far(other).start()
-    for other in range(1, rows):
-        slot = (row + other) % rows
-        pltpu.make_async_copy(far_sum.at[slot], far_sum.at[slot], far_recv.at[slot]).wait()
-    total = far_sum[0]
-    for slot in range(1, rows):
-        total = total + far_sum[slot]
-    out_ref[...] = total
+            src_ref=total_of.at[linear], dst_ref=total_of.at[linear], send_sem=tell_send,
+            recv_sem=tell_recv, device_id=at(target // columns, target % columns), device_id_type=MESH,
+        )
+
+    @pl.loop(1, everyone)
+    def _(other):
+        tell(other).start()
 
     for source in range(chips):
 
@@ -405,23 +428,27 @@
 
     @pl.when(is_home & ends)
     def _():
-        @pl.loop(0, parts)
+        @pl.loop(half, parts)
         def _(part):
             c_first(farthest, part, 1).wait_send()
 
     for kind in range(CORES):
         for order in range(2):
 
-            @pl.when(relays(kind, wanted[order]))
-            def _():
-                @pl.loop(0, parts)
-                def _(part):
+            @pl.loop(0, parts)
+            def _(part):
+                @pl.when(relays(kind, wanted[order], part))
+                def _():
                     c_next(kind, cid(wanted[order], kind, part)).wait_send()
 
-    for other in range(1, rows):
-        far(other).wait_send()
-    for other in range(1, columns):
-        near(other).wait_send()
+    others = total_of.at[pl.ds(1, everyone - 1)]
+    pltpu.make_async_copy(others, others, tell_recv).wait()
+    for i in range(2):
+        totals = [total_of[slot] for slot in range(i, everyone, 2)]
+        while len(totals) > 1:
+            totals = [one + two for one, two in zip(totals[::2], totals[1::2])]
+        out_ref[i] = totals[0]
+    pltpu.make_async_copy(others, others, tell_send).wait()
 
 
 def fused(pair_states, screening, qp_energy, band_energy, band_index, nodes, node_weights):
@@ -433,9 +460,9 @@
     chips = columns // CORES
     mine = width // LANES
     dma = pltpu.SemaphoreType.DMA
-    contrib = pl.pallas_call(
+    halves = pl.pallas_call(
         functools.partial(kernel, rows, columns),
-        out_shape=jax.ShapeDtypeStruct(shape, jnp.float32),
+        out_shape=jax.ShapeDtypeStruct((2,) + shape, jnp.float32),
         in_specs=[pl.BlockSpec(memory_space=pl.ANY)] * 7,
         out_specs=pl.BlockSpec(memory_space=pltpu.VMEM),
         scratch_shapes=[
@@ -445,15 +472,14 @@
             pltpu.VMEM((pairs, LANES), jnp.float32),
             pltpu.VMEM((freqs, pairs, LANES), jnp.float32),
             pltpu.VMEM((LANES, LANES), jnp.float32),
-            pltpu.VMEM((columns,) + shape, jnp.float32),
-            pltpu.VMEM((rows,) + shape, jnp.float32),
+            pltpu.VMEM((rows * columns,) + shape, jnp.float32),
             pltpu.SMEM(qp_energy.shape, jnp.float32),
             pltpu.SMEM(band_energy.shape, jnp.float32),
             pltpu.SMEM(band_index.shape, jnp.int32),
             pltpu.SMEM(nodes.shape, jnp.float32),
             pltpu.SMEM(node_weights.shape, jnp.float32),
-            pltpu.SMEM((columns * freqs + freqs + 2,), jnp.int32),
-            pltpu.SMEM((columns * freqs + freqs + 2,), jnp.int32),
+            pltpu.SMEM(((columns + 2) * freqs + 2,), jnp.int32),
+            pltpu.SMEM(((columns + 2) * freqs + 2,), jnp.int32),
             dma((5,)),
             dma((RING,)),
             dma((parts,)),
@@ -462,10 +488,8 @@
             dma((2, chips * parts)),
             dma((mine,)),
             dma((mine,)),
-            dma((columns,)),
-            dma((columns,)),
-            dma((rows,)),
-            dma((rows,)),
+            dma,
+            dma,
         ],
         compiler_params=pltpu.CompilerParams(
             collective_id=0, has_side_effects=True, vmem_limit_bytes=67043328
@@ -476,6 +500,7 @@
             transcendentals=0,
         ),
     )(pair_states, screening, qp_energy, band_energy, band_index, nodes, node_weights)
+    contrib = halves[0] + halves[1]
     return contrib, jnp.sum(contrib, axis=1)
 
 

time: 114 us -> 103 us (0.904)
  Pallas kernels: 111 us -> 100 us
  local copies, waits for them, and re-layouts: 1.27 us -> 0 us
    pallas_call x1, Pallas kernels: 111 us -> 100 us  [fused(): pl.pallas_call(functools.partial(kernel, rows, columns), out_shape=jax.Sh...]
    unnamed x1 -> x0, local copies, waits for them, and re-layouts: 1.27 us -> none
where the time goes in v2:
time: 103 us
  Pallas kernels  100 us (97%)
  other arithmetic  1.9 us (2%)
    pallas_call x1, Pallas kernels, fused(): pl.pallas_call(functools.partial(kernel, rows, columns), out_shape=jax.Sh...  100 us

profile of v2, /device:TPU:0, one launch (start us, length us, event | category | flops | bytes accessed | tf_op | source)
XLA Modules:
  0.0 102.6 jit_solution(9671890222645115845)
XLA Ops:
  0.6 100.0 %shard_map.86 = f32[2,8,128]{2,1,0:T(8,128)} custom-call(bf16[1024,512]{1,0:T(8,128)(2,1)} %own_ref.1, bf16[4,4096,2048]{2,1,0:T(8,128)(2,1)} %w_ref.1, f32[8]{0:T(128)} %qp_ref.1, f32[2048]{0:T(1024)} %band_ref.1, s32[128]{0:T(128)} %index_ref.1, f32[4]{0:T(128)} %nodes_ref.1, f32[4]{0:T(128)} %weights_ref.1), custom_call_target="tpu_custom_call" | custom-call | flops 68719476736 | bytes 67108864 | tf_op jit(solution)/shard_map/pallas_call | solution.py:463
  100.7 1.9 %fusion = (f32[8]{0:T(128)}, f32[8,128]{1,0:T(8,128)}) fusion(f32[2,8,128]{2,1,0:T(8,128)} %shard_map.86), kind=kLoop, calls=%fused_computation.1 | loop fusion | flops 2040 | bytes 12320 | tf_op jit(solution)/shard_map/reduce_sum | solution.py:504
